TPU v7x, 16 devices: a whole 2x2x2 slice. The times are simulated.
16 devices in a mesh: cp: 16 (over z, y, x, core).
Axes of the slice: x: 2, y: 2, z: 2, core: 2. Of those that a mesh axis runs over, the one named last changes fastest.
Arguments:
- queries: bfloat16 [1024, 128, 192], P('cp')
- latent: bfloat16 [1024, 512], P('cp')
- key_rope: bfloat16 [1024, 64], P('cp')
- w_uk: bfloat16 [512, 128, 128], replicated
- w_uv: bfloat16 [512, 128, 128], replicated
- d_out: bfloat16 [1024, 128, 128], P('cp')
Outputs:
- output 1: bfloat16 [1024, 128, 128], P('cp')
- output 2: bfloat16 [1024, 128, 192], P('cp')
- output 3: bfloat16 [1024, 512], P('cp')
- output 4: bfloat16 [1024, 64], P('cp')
- output 5: float32 [512, 128, 128], replicated
- output 6: float32 [512, 128, 128], replicated
All inputs are finite; a program needn't handle non-finite values.
Results may differ from a plain program's by a relative error of at most 0.0167186.
Values are sent between devices in bfloat16 or wider.
A program may use at most 1 GiB of HBM per device.

v0:
```python
import math
import jax
import jax.numpy as jnp
from jax import lax
from jax.sharding import PartitionSpec as P


def solution(mesh):
    n_dev = mesh.shape["cp"]
    seq_spec = P("cp")

    def gather_all(k_nope, values, key_rope):
        k_all = lax.all_gather(k_nope, "cp", tiled=True)
        v_all = lax.all_gather(values, "cp", tiled=True)
        r_all = lax.all_gather(key_rope, "cp", tiled=True)
        return k_all, v_all, r_all

    def local_step(queries, latent, key_rope, w_uk, w_uv, d_out):
        tok_count = queries.shape[0]
        nope_dim = w_uk.shape[-1]
        score_scale = 1.0 / math.sqrt(queries.shape[-1])
        dev_index = lax.axis_index("cp")
        q_nope = queries[:, :, :nope_dim]
        q_rope = queries[:, :, nope_dim:]
        q_pos = dev_index * tok_count + jnp.arange(tok_count)
        visible = jnp.arange(tok_count * n_dev)[None, :] <= q_pos[:, None]

        def masked_scores(k_all, r_all):
            scores = (jnp.einsum("qhd,khd->hqk", q_nope, k_all, preferred_element_type=jnp.float32)
                      + jnp.einsum("qhd,kd->hqk", q_rope, r_all, preferred_element_type=jnp.float32)) * score_scale
            return jnp.where(visible[None], scores, -1e30)

        k_nope = jnp.einsum("tl,lhd->thd", latent, w_uk, preferred_element_type=jnp.float32).astype(jnp.bfloat16)
        values = jnp.einsum("tl,lhd->thd", latent, w_uv, preferred_element_type=jnp.float32).astype(jnp.bfloat16)

        k_all, v_all, r_all = gather_all(k_nope, values, key_rope)
        scores = masked_scores(k_all, r_all)
        row_max = jnp.max(scores, axis=-1, keepdims=True)
        exp_scores = jnp.exp(scores - row_max)
        row_sum = jnp.sum(exp_scores, axis=-1, keepdims=True)
        log_norm = row_max + jnp.log(row_sum)
        fwd_prob = (exp_scores / row_sum).astype(jnp.bfloat16)
        attn_out = jnp.einsum("hqk,khd->qhd", fwd_prob, v_all, preferred_element_type=jnp.float32).astype(jnp.bfloat16)

        k_all, v_all, r_all = gather_all(k_nope, values, key_rope)
        attn_prob = jnp.exp(masked_scores(k_all, r_all) - log_norm)
        prob_b = attn_prob.astype(jnp.bfloat16)
        d_prob = jnp.einsum("qhd,khd->hqk", d_out, v_all, preferred_element_type=jnp.float32)
        row_delta = jnp.einsum("qhd,qhd->hq", d_out, attn_out, preferred_element_type=jnp.float32)[:, :, None]
        d_score = (attn_prob * (d_prob - row_delta) * score_scale).astype(jnp.bfloat16)
        d_q_nope = jnp.einsum("hqk,khd->qhd", d_score, k_all, preferred_element_type=jnp.float32)
        d_q_rope = jnp.einsum("hqk,kd->qhd", d_score, r_all, preferred_element_type=jnp.float32)
        d_query = jnp.concatenate([d_q_nope, d_q_rope], axis=-1).astype(jnp.bfloat16)
        dk_part = jnp.einsum("hqk,qhd->khd", d_score, q_nope, preferred_element_type=jnp.float32).astype(jnp.bfloat16)
        dv_part = jnp.einsum("hqk,qhd->khd", prob_b, d_out, preferred_element_type=jnp.float32).astype(jnp.bfloat16)
        dr_part = jnp.einsum("hqk,qhd->kd", d_score, q_rope, preferred_element_type=jnp.float32).astype(jnp.bfloat16)
        d_k_nope = lax.psum_scatter(dk_part, "cp", scatter_dimension=0, tiled=True)
        d_values = lax.psum_scatter(dv_part, "cp", scatter_dimension=0, tiled=True)
        d_key_rope = lax.psum_scatter(dr_part, "cp", scatter_dimension=0, tiled=True)
        d_latent = (jnp.einsum("thd,lhd->tl", d_k_nope, w_uk, preferred_element_type=jnp.float32)
                    + jnp.einsum("thd,lhd->tl", d_values, w_uv, preferred_element_type=jnp.float32)).astype(jnp.bfloat16)
        d_w_uk = lax.psum(jnp.einsum("tl,thd->lhd", latent, d_k_nope, preferred_element_type=jnp.float32), "cp")
        d_w_uv = lax.psum(jnp.einsum("tl,thd->lhd", latent, d_values, preferred_element_type=jnp.float32), "cp")
        return attn_out, d_query, d_latent, d_key_rope, d_w_uk, d_w_uv

    return jax.shard_map(local_step, mesh=mesh,
                         in_specs=(seq_spec, seq_spec, seq_spec, P(), P(), seq_spec),
                         out_specs=(seq_spec, seq_spec, seq_spec, seq_spec, P(), P()),
                         check_vma=False)
```

profile of v0, /device:TPU:0, one launch (start us, length us, event | category | flops | bytes accessed | tf_op | source)
XLA Modules:
  0.0 1709.8 jit_solution(15497911076114857605)
XLA Ops:
  7.2 0.0 all-gather.5.cloned.1.call-start
  7.2 24.6 %copy.61 = bf16[512,128,128]{0,2,1:T(8,128)(2,1)} copy(bf16[512,128,128]{2,1,0:T(8,128)(2,1)} %param.9) | data formatting | bytes 33554432 | tf_op args[3]
  31.8 10.2 convolution_convert_fusion
  42.1 0.0 all-gather.3.cloned.1.call-start
  42.1 24.7 %copy.63 = bf16[512,128,128]{0,2,1:T(8,128)(2,1)} copy(bf16[512,128,128]{2,1,0:T(8,128)(2,1)} %param.10) | data formatting | bytes 33554432 | tf_op args[4]
  66.8 10.2 convolution_convert_fusion.1
  77.1 0.0 reduce-scatter.6.cloned.1.call-start
  77.1 1.3 slice.7
  78.4 3.2 slice.6
  81.6 3.7 copy.65
  85.3 3.3 copy.69
  88.6 16.7 all_gather.14
  105.4 0.1 iota_compare_fusion
  105.5 83.7 %all-gather.5.cloned.1.call-done = bf16[1024,128,128]{2,0,1:T(8,128)(2,1)} async-done(((bf16[64,128,128]{2,0,1:T(8,128)(2,1)}), bf16[1024,128,128]{2,0,1:T(8,128)(2,1)}) %all-gather.5.cloned.1.call-update) | async-done | bytes 33554448 | tf_op jit(solution)/shard_map/all_gather | solution.py:13
  189.2 25.0 %fusion.23 = f32[128,1024,64]{1,2,0:T(8,128)} fusion(bf16[1024,128,128]{2,0,1:T(8,128)(2,1)} %all-gather.5.cloned.1.call-done, bf16[64,128,128]{2,0,1:T(8,128)(2,1)S(1)} %copy.69), kind=kOutput, calls=%fused_computation.44 | convolution fusion | flops 2147483648 | bytes 69206016 | tf_op jit(solution)/shard_map/qhd,khd->hqk/dot_general | solution.py:29
  214.2 22.6 %fusion.22 = (f32[128,64]{1,0:T(8,128)S(1)}, f32[128,64,1024]{2,1,0:T(8,128)}) fusion(bf16[64,128,64]{2,0,1:T(8,128)(2,1)} %copy.65, bf16[1024,64]{1,0:T(8,128)(2,1)S(1)} %all_gather.14, f32[128,1024,64]{1,2,0:T(8,128)} %fusion.23, pred[64,1024]{1,0:T(8,128)(4,1)S(1)} %iota_compare_fusion), kind=kOutput, calls=%fused_computation.43 | convolution fusion | flops 1107288064 | bytes 68386816 | tf_op jit(solution)/shard_map/qhd,kd->hqk/dot_general | solution.py:30
  236.8 13.8 fusion.4
  250.6 26.6 %convert_bitcast_fusion = bf16[1024,128,128]{2,0,1:T(8,128)(2,1)} fusion(f32[128,64,1024]{2,1,0:T(8,128)} %get-tuple-element.21, f32[128,64]{1,0:T(8,128)S(1)} %log_add_fusion, bf16[64,128,128]{2,1,0:T(8,128)(2,1)S(1)} %copy-done.3), kind=kOutput, calls=%fused_computation.6 | convolution fusion | flops 2181038080 | bytes 69238784 | tf_op jit(solution)/shard_map/hqk,qhd->khd/dot_general | solution.py:55
  277.2 0.0 reduce-scatter.6.cloned.1.call-update
  277.2 0.2 reduce-scatter.4.cloned.1.call-start
  277.4 58.1 %all-gather.3.cloned.1.call-done = bf16[1024,128,128]{2,0,1:T(8,128)(2,1)} async-done(((bf16[64,128,128]{2,0,1:T(8,128)(2,1)}), bf16[1024,128,128]{2,0,1:T(8,128)(2,1)}) %all-gather.3.cloned.1.call-update) | async-done | bytes 33554448 | tf_op jit(solution)/shard_map/all_gather | solution.py:14
  335.5 25.7 %bitcast_convert_fusion = (f32[128,64,128]{2,1,0:T(8,128)}, bf16[128,128,64]{1,2,0:T(8,128)(2,1)}) fusion(bf16[1024,128,128]{2,0,1:T(8,128)(2,1)} %all-gather.3.cloned.1.call-done, f32[128,64,1024]{2,1,0:T(8,128)} %get-tuple-element.21, f32[128,64]{1,0:T(8,128)S(1)} %fusion.4, f32[128,64]{1,0:T(8,128)S(1)} %get-tuple-element.20), kind=kOutput, calls=%fused_computation.19 | convolution fusion | flops 2174746624 | bytes 73465856 | tf_op jit(solution)/shard_map/hqk,khd->qhd/dot_general | solution.py:43
  361.2 4.6 multiply_reduce_fusion
  365.8 0.1 copy.56
  365.9 29.4 %fusion.1 = bf16[128,64,1024]{2,1,0:T(8,128)(2,1)} fusion(f32[128,64,1024]{2,1,0:T(8,128)} %get-tuple-element.21, f32[128,64]{1,0:T(8,128)S(1)} %copy.56, f32[128,64]{1,0:T(8,128)S(1)} %log_add_fusion, bf16[1024,128,128]{2,0,1:T(8,128)(2,1)} %all-gather.3.cloned.1.call-done, bf16[64,128,128]{2,1,0:T(8,128)(2,1)} %param.11), kind=kOutput, calls=%fused_computation.2 | convolution fusion | flops 2189426688 | bytes 86048768 | tf_op jit(solution)/shard_map/qhd,khd->hqk/dot_general | solution.py:48
  395.2 20.1 %convert_bitcast_fusion.1 = bf16[1024,128,128]{2,0,1:T(8,128)(2,1)} fusion(bf16[128,64,1024]{2,1,0:T(8,128)(2,1)} %fusion.1, bf16[64,128,128]{2,0,1:T(8,128)(2,1)S(1)} %copy-done.2), kind=kOutput, calls=%fused_computation.7 | convolution fusion | flops 2164260864 | bytes 52428800 | tf_op jit(solution)/shard_map/hqk,qhd->khd/dot_general | solution.py:54
  415.3 0.0 reduce-scatter.4.cloned.1.call-update
  415.3 0.0 all-reduce.3.cloned.1.call-start
  415.4 268.9 %reduce-scatter.6.cloned.1.call-done = bf16[64,128,128]{2,0,1:T(8,128)(2,1)} async-done(((bf16[1024,128,128]{2,0,1:T(8,128)(2,1)}), bf16[64,128,128]{2,0,1:T(8,128)(2,1)}) %reduce-scatter.6.cloned.1.call-update) | async-done | bytes 2097168 | tf_op jit(solution)/shard_map/reduce_scatter | solution.py:58
  684.3 15.6 convolution_bitcast_fusion
  699.9 331.2 %reduce-scatter.4.cloned.1.call-done = bf16[64,128,128]{2,0,1:T(8,128)(2,1)} async-done(((bf16[1024,128,128]{2,0,1:T(8,128)(2,1)}), bf16[64,128,128]{2,0,1:T(8,128)(2,1)}) %reduce-scatter.4.cloned.1.call-update) | async-done | bytes 2097168 | tf_op jit(solution)/shard_map/reduce_scatter | solution.py:57
  1031.1 15.6 convolution_bitcast_fusion.1
  1046.7 0.0 all-reduce.3.cloned.1.call-update
  1046.8 0.3 reduce-scatter.8.cloned.1.call-start
  1047.0 1.3 copy-done.5
  1048.3 2.7 copy.44
  1051.0 8.3 fusion.15
  1059.3 2.2 copy.59
  1061.5 3.7 copy.37
  1065.2 18.5 %convert_bitcast_fusion.2 = bf16[64,128,128]{2,0,1:T(8,128)(2,1)S(1)} fusion(bf16[128,64,1024]{2,1,0:T(8,128)(2,1)} %fusion.1, bf16[1024,128,128]{2,0,1:T(8,128)(2,1)} %all-gather.5.cloned.1.call-done), kind=kOutput, calls=%fused_computation.20 | convolution fusion | flops 2148532224 | bytes 52428800 | tf_op jit(solution)/shard_map/hqk,khd->qhd/dot_general | solution.py:51
  1083.7 5.1 pad_maximum_fusion
  1088.8 6.8 copy.45
  1095.6 11.6 fusion.12
  1107.2 8.1 convolution_bitcast_fusion.4
  1115.4 8.0 fusion.14
  1123.4 508.3 %all-reduce.3.cloned.1.call-done = (f32[512,128,128]{0,2,1:T(8,128)}, f32[512,128,128]{0,2,1:T(8,128)}) async-done(((f32[512,128,128]{0,2,1:T(8,128)}, f32[512,128,128]{0,2,1:T(8,128)}), (f32[512,128,128]{0,2,1:T(8,128)}, f32[512,128,128]{0,2,1:T(8,128)})) %all-reduce.3.cloned.1.call-update) | async-done | bytes 67108880 | tf_op jit(solution)/shard_map/psum | solution.py:62
  1631.7 35.4 %copy.46 = f32[512,128,128]{2,1,0:T(8,128)} copy(f32[512,128,128]{0,2,1:T(8,128)} %get-tuple-element.18) | data formatting | bytes 67108864
  1667.1 35.4 %copy.47 = f32[512,128,128]{2,1,0:T(8,128)} copy(f32[512,128,128]{0,2,1:T(8,128)} %get-tuple-element.19) | data formatting | bytes 67108864
  (23 shorter events, 0.1 us)
Async XLA Ops:
  7.2 24.6 %copy-start = (bf16[64,512]{1,0:T(8,128)(2,1)S(1)}, bf16[64,512]{1,0:T(8,128)(2,1)}, u32[]{:S(2)}) copy-start(bf16[64,512]{1,0:T(8,128)(2,1)} %param.7) | copy-start | bytes 196612
  7.2 182.1 %all-gather.5.cloned.1.call-start = ((), (), s32[]{:S(2)}) async-start(), calls=%async_computation.4 | async-start | bytes 35651584 | tf_op jit(solution)/shard_map/all_gather | solution.py:13
  42.1 293.4 %all-gather.3.cloned.1.call-start = ((), (), s32[]{:S(2)}) async-start(), calls=%async_computation.3 | async-start | bytes 35651584 | tf_op jit(solution)/shard_map/all_gather | solution.py:14
  66.8 21.8 %copy-start.8 = (bf16[64,64]{1,0:T(8,128)(2,1)S(1)}, bf16[64,64]{1,0:T(8,128)(2,1)}, u32[]{:S(2)}) copy-start(bf16[64,64]{1,0:T(8,128)(2,1)} %param.8) | copy-start | bytes 24580
  77.1 607.2 %reduce-scatter.6.cloned.1.call-start = ((), (), s32[]{:S(2)}) async-start(), calls=%async_computation.6 | async-start | bytes 35651584 | tf_op jit(solution)/shard_map/reduce_scatter | solution.py:58
  88.6 125.6 %copy-start.1 = (bf16[64,128,128]{2,0,1:T(8,128)(2,1)}, bf16[64,128,128]{2,0,1:T(8,128)(2,1)S(1)}, u32[]{:S(2)}) copy-start(bf16[64,128,128]{2,0,1:T(8,128)(2,1)S(1)} %copy.69) | copy-start | bytes 6291460
  105.4 108.8 %copy-start.6 = (bf16[1024,64]{1,0:T(8,128)(2,1)}, bf16[1024,64]{1,0:T(8,128)(2,1)S(1)}, u32[]{:S(2)}) copy-start(bf16[1024,64]{1,0:T(8,128)(2,1)S(1)} %all_gather.14) | copy-start | bytes 393220
  236.8 13.8 copy-start.3
  277.2 753.9 %reduce-scatter.4.cloned.1.call-start = ((), (), s32[]{:S(2)}) async-start(), calls=%async_computation.5 | async-start | bytes 35651584 | tf_op jit(solution)/shard_map/reduce_scatter | solution.py:57
  365.8 29.4 %copy-start.2 = (bf16[64,128,128]{2,0,1:T(8,128)(2,1)S(1)}, bf16[64,128,128]{2,0,1:T(8,128)(2,1)}, u32[]{:S(2)}) copy-start(bf16[64,128,128]{2,0,1:T(8,128)(2,1)} %copy-done.1) | copy-start | bytes 6291460
  415.3 1216.3 %all-reduce.3.cloned.1.call-start = ((), (), s32[]{:S(2)}) async-start(), calls=%async_computation.8 | async-start | bytes 134217728 | tf_op jit(solution)/shard_map/psum | solution.py:62
  1046.7 1.6 copy-start.5
  1046.7 4.3 copy-start.7
  1046.8 655.8 %reduce-scatter.8.cloned.1.call-start = ((), (), s32[]{:S(2)}) async-start(), calls=%async_computation.7 | async-start | bytes 278528 | tf_op jit(solution)/shard_map/reduce_scatter | solution.py:59
  1107.2 8.1 copy-start.4
Sparse Core Ops, SparseCore 0:
  42.2 147.0 all-gather.4
  192.1 143.3 all-gather.2
  338.4 345.7 reduce-scatter.5
  687.0 344.0 reduce-scatter.3
  1046.9 584.7 all-reduce.2
  1634.3 54.1 reduce-scatter.7
where the time goes:
time: 1720 us; the launch traced here: 1710 us
  waiting for transfers between devices  1250 us (73%)
  matrix products  255 us (15%)
  local copies, waits for them, and re-layouts  148 us (9%)
  other arithmetic  23.6 us (1%)
    psum x1, waiting for transfers between devices, local_step(): lax.psum(jnp.einsum('tl,thd->lhd', latent, d_k_nope, preferred_element_ty...  508 us
    reduce_scatter x1, waiting for transfers between devices, local_step(): d_k_nope = lax.psum_scatter(dk_part, 'cp', scatter_dimension=0, tiled=True)  331 us
    reduce_scatter x1, waiting for transfers between devices, local_step(): d_values = lax.psum_scatter(dv_part, 'cp', scatter_dimension=0, tiled=True)  269 us
    unnamed x25, local copies, waits for them, and re-layouts  134 us
    all_gather x1, waiting for transfers between devices, gather_all(): k_all = lax.all_gather(k_nope, 'cp', tiled=True)  83.7 us
    all_gather x1, waiting for transfers between devices, gather_all(): v_all = lax.all_gather(values, 'cp', tiled=True)  58.1 us
  transfers between devices with their start and end apart: 6, of which 5 were waited for; matrix products, arithmetic and copies ran while one was open for 22% of the time, Pallas kernels for 0%

commit v1 on v0

v1 whole, which is shorter than its diff:
```python
import functools
import math
import jax
import jax.numpy as jnp
from jax import lax
from jax.experimental import pallas as pl
from jax.experimental.pallas import tpu as pltpu
from jax.sharding import PartitionSpec as P

N_CHUNK = 4
Q_BLK = 256
LOG2E = 1.4426950408889634
F32 = jnp.float32
BF16 = jnp.bfloat16


def dot(a, b):
    return lax.dot_general(a, b, (((1,), (0,)), ((), ())), preferred_element_type=F32)


def dot_t(a, b):
    return lax.dot_general(a, b, (((1,), (1,)), ((), ())), preferred_element_type=F32)


def head_kernel(scale, x_ref, c_ref, ra_ref, rb_ref, wk_ref, wv_ref, dkv_ref, dr_ref, kx_ref, v_ref, q_ref, p_ref, ds_ref):
    n_src, _, tok, width = x_ref.shape
    seq = n_src * tok
    n_blk = seq // Q_BLK
    scale2 = scale * LOG2E
    x = x_ref[...].reshape(seq, width)
    c = c_ref[...]
    k_all = dot(c, jnp.concatenate([wk_ref[0], wk_ref[1]], axis=-1)).astype(BF16)
    v_all = dot(c, jnp.concatenate([wv_ref[0], wv_ref[1]], axis=-1)).astype(BF16)
    v_ref[...] = v_all
    lane = lax.broadcasted_iota(jnp.int32, (Q_BLK, 128), 1)
    for a in range(2):
        cols = slice(a * 128, (a + 1) * 128)
        kx_ref[...] = jnp.concatenate([k_all[:, cols], (ra_ref, rb_ref)[a][...]], axis=-1)
        q_ref[...] = jnp.concatenate([x[:, cols], x[:, 512:640]], axis=-1)
        do = x[:, 256 + a * 128:384 + a * 128]
        for i in range(n_blk):
            top = (i + 1) * Q_BLK
            rows = slice(i * Q_BLK, top)
            s = dot_t(kx_ref[:top, :], q_ref[rows, :]) * scale2
            key = lax.broadcasted_iota(jnp.int32, (top, Q_BLK), 0)
            qry = lax.broadcasted_iota(jnp.int32, (top, Q_BLK), 1) + i * Q_BLK
            s = jnp.where(key <= qry, s, -1e30)
            e = jnp.exp2(s - jnp.max(s, axis=0, keepdims=True))
            p = e / jnp.sum(e, axis=0, keepdims=True)
            dp = dot_t(v_ref[:top, cols], do[rows, :])
            delta = jnp.sum(p * dp, axis=0, keepdims=True)
            p_ref[:top, rows] = p.astype(BF16)
            ds_ref[:top, rows] = (p * (dp - delta) * scale).astype(BF16)
        for j in range(n_blk):
            rows = slice(j * Q_BLK, (j + 1) * Q_BLK)
            dkv_ref[0, 1, rows, cols] = dot(p_ref[rows, j * Q_BLK:], do[j * Q_BLK:, :]).astype(BF16)
            dk = dot(ds_ref[rows, j * Q_BLK:], q_ref[j * Q_BLK:, :])
            dkv_ref[0, 0, rows, cols] = dk[:, :128].astype(BF16)
            half = dk[:, 128:]
            if a == 0:
                dr_ref[0, rows, :] = half
            else:
                dr_ref[0, rows, :] = jnp.where(lane < 64, dr_ref[0, rows, :], half)


def head_part(scale, x, c, ra, rb, wk, wv):
    n_src, pairs, tok, width = x.shape
    seq = n_src * tok
    full = lambda s: pl.BlockSpec(s, lambda p: (0,) * len(s))
    return pl.pallas_call(
        functools.partial(head_kernel, scale),
        grid=(pairs,),
        in_specs=[
            pl.BlockSpec((n_src, 1, tok, width), lambda p: (0, p, 0, 0)),
            full(c.shape), full(ra.shape), full(rb.shape),
            pl.BlockSpec((2, 512, 128), lambda p: (p, 0, 0)),
            pl.BlockSpec((2, 512, 128), lambda p: (p, 0, 0)),
        ],
        out_specs=[
            pl.BlockSpec((1, 2, seq, 256), lambda p: (p, 0, 0, 0)),
            pl.BlockSpec((1, seq, 128), lambda p: (p, 0, 0)),
        ],
        out_shape=[
            jax.ShapeDtypeStruct((pairs, 2, seq, 256), BF16),
            jax.ShapeDtypeStruct((pairs, seq, 128), F32),
        ],
        scratch_shapes=[
            pltpu.VMEM((seq, 256), BF16), pltpu.VMEM((seq, 256), BF16), pltpu.VMEM((seq, 256), BF16),
            pltpu.VMEM((seq, seq), BF16), pltpu.VMEM((seq, seq), BF16),
        ],
        cost_estimate=pl.CostEstimate(flops=6_000_000_000 * pairs // 2, bytes_accessed=8_000_000, transcendentals=0),
        name="head_part",
    )(x, c, ra, rb, wk, wv)


def query_kernel(scale, x_ref, c_ref, ra_ref, rb_ref, wk_ref, wv_ref, o_ref, dq_ref):
    tok = x_ref.shape[1]
    seq = c_ref.shape[0]
    scale2 = scale * LOG2E
    c = c_ref[...]
    k_all = dot(c, jnp.concatenate([wk_ref[0], wk_ref[1]], axis=-1)).astype(BF16)
    v_all = dot(c, jnp.concatenate([wv_ref[0], wv_ref[1]], axis=-1)).astype(BF16)
    me = lax.axis_index("cp")
    key = lax.broadcasted_iota(jnp.int32, (tok, seq), 1)
    qry = lax.broadcasted_iota(jnp.int32, (tok, seq), 0) + me * tok
    rope = None
    for a in range(2):
        cols = slice(a * 128, (a + 1) * 128)
        kx = jnp.concatenate([k_all[:, cols], (ra_ref, rb_ref)[a][...]], axis=-1)
        q = jnp.concatenate([x_ref[0, :, cols], x_ref[0, :, 512:640]], axis=-1)
        do = x_ref[0, :, 256 + a * 128:384 + a * 128]
        s = jnp.where(key <= qry, dot_t(q, kx) * scale2, -1e30)
        e = jnp.exp2(s - jnp.max(s, axis=1, keepdims=True))
        p = e / jnp.sum(e, axis=1, keepdims=True)
        v = v_all[:, cols]
        o_ref[0, :, cols] = dot(p.astype(BF16), v).astype(BF16)
        dp = dot_t(do, v)
        ds = (p * (dp - jnp.sum(p * dp, axis=1, keepdims=True)) * scale).astype(BF16)
        dq = dot(ds, kx)
        dq_ref[0, :, cols] = dq[:, :128].astype(BF16)
        rope = dq[:, 128:] if a == 0 else rope + dq[:, 128:]
    dq_ref[0, :, 256:] = rope.astype(BF16)


def query_part(scale, x, c, ra, rb, wk, wv):
    pairs, tok, width = x.shape
    full = lambda s: pl.BlockSpec(s, lambda p: (0,) * len(s))
    return pl.pallas_call(
        functools.partial(query_kernel, scale),
        grid=(pairs,),
        in_specs=[
            pl.BlockSpec((1, tok, width), lambda p: (p, 0, 0)),
            full(c.shape), full(ra.shape), full(rb.shape),
            pl.BlockSpec((2, 512, 128), lambda p: (p, 0, 0)),
            pl.BlockSpec((2, 512, 128), lambda p: (p, 0, 0)),
        ],
        out_specs=[
            pl.BlockSpec((1, tok, 256), lambda p: (p, 0, 0)),
            pl.BlockSpec((1, tok, 384), lambda p: (p, 0, 0)),
        ],
        out_shape=[
            jax.ShapeDtypeStruct((pairs, tok, 256), BF16),
            jax.ShapeDtypeStruct((pairs, tok, 384), BF16),
        ],
        cost_estimate=pl.CostEstimate(flops=60_000_000_000, bytes_accessed=50_000_000, transcendentals=0),
        name="query_part",
    )(x, c, ra, rb, wk, wv)


def weight_kernel(tok, n_in, *refs):
    dkv_ref, ct_ref, wk_ref, wv_ref = refs[:4]
    dwk_ref, dwv_ref, dc_ref = refs[n_in:n_in + 3]
    me = lax.axis_index("cp")
    n_pair = dkv_ref.shape[0]
    own = pl.ds(pl.multiple_of(me * tok, tok), tok)
    dc = jnp.zeros(dc_ref.shape, F32)
    for which, (w_ref, out_ref) in enumerate(((wk_ref, dwk_ref), (wv_ref, dwv_ref))):
        flat = out_ref.reshape(512 * 8, 128)
        for p in range(n_pair):
            g = dkv_ref[p, which]
            for m in range(4):
                res = dot(ct_ref[m * 128:(m + 1) * 128, :], g)
                for a in range(2):
                    flat[pl.ds(m * 1024 + 2 * p + a, 128, stride=8), :] = res[:, a * 128:(a + 1) * 128]
            mine = dkv_ref[p, which, own, :]
            dc += dot_t(mine, jnp.concatenate([w_ref[2 * p], w_ref[2 * p + 1]], axis=-1))

    @pl.when(pl.program_id(0) == 0)
    def _():
        dc_ref[...] = dc

    @pl.when(pl.program_id(0) > 0)
    def _():
        dc_ref[...] += dc


def weight_part(tok, first, dkv, ct, wk, wv, prev):
    pairs, _, seq, _ = dkv.shape
    steps = pairs // 4
    base = first // 8
    out_block = pl.BlockSpec((512, 8, 128), lambda g: (0, base + g, 0))
    in_specs = [
        pl.BlockSpec((4, 2, seq, 256), lambda g: (g, 0, 0, 0)),
        pl.BlockSpec((512, seq), lambda g: (0, 0)),
        pl.BlockSpec((8, 512, 128), lambda g: (base + g, 0, 0)),
        pl.BlockSpec((8, 512, 128), lambda g: (base + g, 0, 0)),
    ]
    args = [dkv, ct, wk, wv]
    aliases = {}
    if prev is not None:
        in_specs += [pl.BlockSpec(memory_space=pl.ANY)] * 2
        args += list(prev)
        aliases = {4: 0, 5: 1}
    return pl.pallas_call(
        functools.partial(weight_kernel, tok, len(args)),
        grid=(steps,),
        in_specs=in_specs,
        out_specs=[out_block, out_block, pl.BlockSpec((tok, 512), lambda g: (0, 0))],
        out_shape=[
            jax.ShapeDtypeStruct((512, 128, 128), F32),
            jax.ShapeDtypeStruct((512, 128, 128), F32),
            jax.ShapeDtypeStruct((tok, 512), F32),
        ],
        input_output_aliases=aliases,
        cost_estimate=pl.CostEstimate(flops=2_200_000_000 * steps, bytes_accessed=10_000_000 * steps, transcendentals=0),
        name="weight_part",
    )(*args)


def solution(mesh):
    n_dev = mesh.shape["cp"]
    seq_spec = P("cp")

    def local_step(queries, latent, key_rope, w_uk, w_uv, d_out):
        tok, heads, qk = queries.shape
        scale = 1.0 / math.sqrt(qk)
        pairs = heads // 2
        me = lax.axis_index("cp")

        def pair_major(a):
            return a.reshape(tok, pairs, -1).transpose(1, 0, 2)

        payload = jnp.concatenate(
            [pair_major(queries[:, :, :128]), pair_major(d_out), pair_major(queries[:, :, 128:])], axis=-1)
        cr = lax.all_gather(jnp.concatenate([latent, key_rope], axis=-1), "cp", tiled=True)
        c_all, r_all = cr[:, :512], cr[:, 512:]
        zero = jnp.zeros_like(r_all)
        ra = jnp.concatenate([r_all, zero], axis=-1)
        rb = jnp.concatenate([zero, r_all], axis=-1)

        per = pairs // (N_CHUNK * n_dev)
        chunked = payload.reshape(N_CHUNK, n_dev, per, tok, 640)
        gathered = []
        dr = None
        for j in range(N_CHUNK):
            x = lax.all_to_all(chunked[j], "cp", 0, 0, tiled=True)
            start = j * (heads // N_CHUNK) + me * (2 * per)
            wk = lax.dynamic_slice_in_dim(w_uk, start, 2 * per, 1).transpose(1, 0, 2)
            wv = lax.dynamic_slice_in_dim(w_uv, start, 2 * per, 1).transpose(1, 0, 2)
            dkv, dr_j = head_part(scale, x, c_all, ra, rb, wk, wv)
            gathered.append(lax.all_gather(dkv, "cp", tiled=True))
            dr_j = jnp.sum(dr_j, axis=0)
            dr = dr_j if dr is None else dr + dr_j
        dr = (dr[:, :64] + dr[:, 64:]).reshape(n_dev, tok, 64)
        d_key_rope = jnp.sum(lax.all_to_all(dr, "cp", 0, 0, tiled=True), axis=0).astype(BF16)

        wk_h = w_uk.transpose(1, 0, 2)
        wv_h = w_uv.transpose(1, 0, 2)
        o_p, dq_p = query_part(scale, payload, c_all, ra, rb, wk_h, wv_h)
        attn_out = o_p.transpose(1, 0, 2).reshape(tok, heads, 128)
        dq_n = dq_p[:, :, :256].transpose(1, 0, 2).reshape(tok, heads, 128)
        dq_r = dq_p[:, :, 256:].transpose(1, 0, 2).reshape(tok, heads, 64)
        d_query = jnp.concatenate([dq_n, dq_r], axis=-1)

        ct = c_all.T
        prev = None
        dc = None
        for j in range(N_CHUNK):
            dwk, dwv, dc_j = weight_part(tok, j * (heads // N_CHUNK), gathered[j], ct, wk_h, wv_h, prev)
            prev = (dwk, dwv)
            dc = dc_j if dc is None else dc + dc_j
        return attn_out, d_query, dc.astype(BF16), d_key_rope, prev[0], prev[1]

    return jax.shard_map(local_step, mesh=mesh,
                         in_specs=(seq_spec, seq_spec, seq_spec, P(), P(), seq_spec),
                         out_specs=(seq_spec, seq_spec, seq_spec, seq_spec, P(), P()),
                         check_vma=False)
```

time: 1720 us -> 498 us (0.29)
  waiting for transfers between devices: 1250 us -> 0.16 us
  Pallas kernels: 0 us -> 273 us
  matrix products: 255 us -> 0 us
  blocking collectives: 16.7 us -> 92.9 us
  local copies, waits for them, and re-layouts: 148 us -> 93.3 us
    reduce_scatter x3 -> x0, waiting for transfers between devices: 600 us -> none  [the longest x1 331 us: local_step(): d_k_nope = lax.psum_scatter(dk_part, 'cp', scatter_dimension=0, tiled=True)]
    psum x1 -> x0, waiting for transfers between devices: 508 us -> none  [local_step(): lax.psum(jnp.einsum('tl,thd->lhd', latent, d_k_nope, preferred_element_ty...]
    pallas_call x0 -> x9, Pallas kernels: none -> 273 us  [the longest x1 162 us: query_part(): pl.pallas_call(functools.partial(query_kernel, scale), grid=(pairs,), in_...]
    dot_general x15 -> x0, matrix products: 255 us -> none  [the longest x1 29.4 us: local_step(): jnp.einsum('qhd,khd->hqk', d_out, v_all, preferred_element_type=jnp.float32)]
    all_gather x2 -> x5, waiting for transfers between devices: 142 us -> 0.07 us  [the longest x4 0.06 us: local_step(): gathered.append(lax.all_gather(dkv, 'cp', tiled=True))]
    all_to_all x0 -> x3, blocking collectives: none -> 92.9 us  [local_step(): x = lax.all_to_all(chunked[j], 'cp', 0, 0, tiled=True)]
    unnamed x25 -> x27, local copies, waits for them, and re-layouts: 134 us -> 45.7 us
  transfers between devices with their start and end apart: 6 -> 7, of which waited for: 5 -> 0; matrix products, arithmetic and copies ran while one was open for 22% -> 16% of each run, Pallas kernels for 0% -> 50%
where the time goes in v1:
time: 498 us; the launch traced here: 493 us
  Pallas kernels  273 us (55%)
  local copies, waits for them, and re-layouts  93.3 us (19%)
  blocking collectives  92.9 us (19%)
  between operations  14.2 us (3%)
  other arithmetic  10.9 us (2%)
  starting transfers between devices  7.99 us (2%)
    pallas_call x1, Pallas kernels, query_part(): pl.pallas_call(functools.partial(query_kernel, scale), grid=(pairs,), in_...  162 us
    all_to_all x3, blocking collectives, local_step(): x = lax.all_to_all(chunked[j], 'cp', 0, 0, tiled=True)  92.9 us
    pallas_call x4, Pallas kernels, weight_part(): pl.pallas_call(functools.partial(weight_kernel, tok, len(args)), grid=(st...  79.2 us
    unnamed x27, local copies, waits for them, and re-layouts  45.7 us
    pallas_call x4, Pallas kernels, head_part(): pl.pallas_call(functools.partial(head_kernel, scale), grid=(pairs,), in_s...  32.4 us
  transfers between devices with their start and end apart: 7, of which 0 were waited for; matrix products, arithmetic and copies ran while one was open for 16% of the time, Pallas kernels for 50%

profile of v1, /device:TPU:0, one launch (start us, length us, event | category | flops | bytes accessed | tf_op | source)
XLA Modules:
  0.0 492.8 jit_solution(4439090145930471281)
XLA Ops:
  7.2 1.6 slice-done
  8.8 2.9 copy.87
  11.6 4.2 reshape.49
  15.8 2.1 reshape.50
  18.0 1.1 copy.90
  19.0 1.0 reshape.51
  20.0 0.7 copy.123
  20.7 4.6 copy_bitcast_fusion
  25.3 0.6 pad_maximum_fusion.x_ref
  26.0 2.4 slice_bitcast_fusion.4
  28.4 0.6 copy-done
  29.0 5.3 %all-to-all-start = ((bf16[16,1,64,640]{3,2,1,0:T(8,128)(2,1)}), bf16[16,1,64,640]{3,2,1,0:T(8,128)(2,1)}, u32[]{:S(2)}, u32[]{:S(2)}) async-start(bf16[16,1,64,640]{3,2,1,0:T(8,128)(2,1)} %get-tuple-element.74), calls=%async_computation | async-start | bytes 2621440 | tf_op jit(solution)/shard_map/all_to_all | solution.py:236
  34.4 0.6 pad_maximum_fusion.2
  35.3 36.6 %fusion = (bf16[512,128,128]{2,0,1:T(8,128)(2,1)}, bf16[128,512,128]{2,1,0:T(8,128)(2,1)}, bf16[128,512,128]{2,1,0:T(8,128)(2,1)}, bf16[512,128,128]{2,0,1:T(8,128)(2,1)}) fusion(bf16[512,128,128]{2,1,0:T(8,128)(2,1)} %param.10, bf16[512,128,128]{2,1,0:T(8,128)(2,1)} %param.9), kind=kLoop, calls=%fused_computation.25 | loop fusion | bytes 100663296 | tf_op args[4]
  71.9 2.2 dynamic-slice_bitcast_fusion.6
  74.1 2.2 dynamic-slice_bitcast_fusion.7
  76.3 2.3 slice.52.c_ref
  78.6 1.0 slice.53
  79.5 0.9 fusion.2
  80.5 8.0 %head_part.4 = (bf16[1,2,1024,256]{3,2,1,0:T(8,128)(2,1)}, f32[1,1024,128]{2,1,0:T(8,128)}) custom-call(bf16[16,1,64,640]{3,2,1,0:T(8,128)(2,1)} %all-to-all-done.x_ref, bf16[1024,512]{1,0:T(8,128)(2,1)} %slice.52.c_ref, bf16[1024,128]{1,0:T(8,128)(2,1)} %get-tuple-element.79.ra_ref, bf16[1024,128]{1,0:T(8,128)(2,1)} %get-tuple-element.78.rb_ref, ...), custom_call_target="tpu_custom_call" | custom-call | flops 3000000000 | bytes 8000000 | tf_op jit(solution)/shard_map/head_part/pallas_call | solution.py:70
  88.6 30.2 %all_to_all.25.x_ref = bf16[16,1,64,640]{3,2,1,0:T(8,128)(2,1)} all-to-all(bf16[16,1,64,640]{3,2,1,0:T(8,128)(2,1)} %get-tuple-element.77), channel_id=1, replica_groups=mesh['cp'=16] {'cp'}, dimensions={0} | all-to-all | bytes 2621440 | tf_op jit(solution)/shard_map/all_to_all | solution.py:236
  118.9 8.1 %head_part.5 = (bf16[1,2,1024,256]{3,2,1,0:T(8,128)(2,1)}, f32[1,1024,128]{2,1,0:T(8,128)}) custom-call(bf16[16,1,64,640]{3,2,1,0:T(8,128)(2,1)} %all_to_all.25.x_ref, bf16[1024,512]{1,0:T(8,128)(2,1)} %slice.52.c_ref, bf16[1024,128]{1,0:T(8,128)(2,1)} %get-tuple-element.79.ra_ref, bf16[1024,128]{1,0:T(8,128)(2,1)} %get-tuple-element.78.rb_ref, ...), custom_call_target="tpu_custom_call" | custom-call | flops 3000000000 | bytes 8000000 | tf_op jit(solution)/shard_map/head_part/pallas_call | solution.py:70
  127.0 26.8 %all_to_all.26.x_ref = bf16[16,1,64,640]{3,2,1,0:T(8,128)(2,1)} all-to-all(bf16[16,1,64,640]{3,2,1,0:T(8,128)(2,1)S(1)} %get-tuple-element.76), channel_id=1, replica_groups=mesh['cp'=16] {'cp'}, dimensions={0} | all-to-all | bytes 2621440 | tf_op jit(solution)/shard_map/all_to_all | solution.py:236
  153.8 8.1 %head_part.6 = (bf16[1,2,1024,256]{3,2,1,0:T(8,128)(2,1)}, f32[1,1024,128]{2,1,0:T(8,128)}) custom-call(bf16[16,1,64,640]{3,2,1,0:T(8,128)(2,1)} %all_to_all.26.x_ref, bf16[1024,512]{1,0:T(8,128)(2,1)} %slice.52.c_ref, bf16[1024,128]{1,0:T(8,128)(2,1)} %get-tuple-element.79.ra_ref, bf16[1024,128]{1,0:T(8,128)(2,1)} %get-tuple-element.78.rb_ref, ...), custom_call_target="tpu_custom_call" | custom-call | flops 3000000000 | bytes 8000000 | tf_op jit(solution)/shard_map/head_part/pallas_call | solution.py:70
  162.0 35.8 %all_to_all.27.x_ref = bf16[16,1,64,640]{3,2,1,0:T(8,128)(2,1)} all-to-all(bf16[16,1,64,640]{3,2,1,0:T(8,128)(2,1)S(1)} %get-tuple-element.75), channel_id=1, replica_groups=mesh['cp'=16] {'cp'}, dimensions={0} | all-to-all | bytes 2621440 | tf_op jit(solution)/shard_map/all_to_all | solution.py:236
  197.8 8.2 %head_part.7 = (bf16[1,2,1024,256]{3,2,1,0:T(8,128)(2,1)}, f32[1,1024,128]{2,1,0:T(8,128)}) custom-call(bf16[16,1,64,640]{3,2,1,0:T(8,128)(2,1)} %all_to_all.27.x_ref, bf16[1024,512]{1,0:T(8,128)(2,1)} %slice.52.c_ref, bf16[1024,128]{1,0:T(8,128)(2,1)} %get-tuple-element.79.ra_ref, bf16[1024,128]{1,0:T(8,128)(2,1)} %get-tuple-element.78.rb_ref, ...), custom_call_target="tpu_custom_call" | custom-call | flops 3000000000 | bytes 8000000 | tf_op jit(solution)/shard_map/head_part/pallas_call | solution.py:70
  206.0 1.1 add_bitcast_fusion
  207.4 1.0 reshape.56
  208.4 2.3 all-to-all-start.4
  210.7 161.8 %query_part.1 = (bf16[64,64,256]{2,1,0:T(8,128)(2,1)}, bf16[64,64,384]{2,1,0:T(8,128)(2,1)}) custom-call(bf16[64,64,640]{2,1,0:T(8,128)(2,1)} %copy-done, bf16[1024,512]{1,0:T(8,128)(2,1)} %slice.52.c_ref, bf16[1024,128]{1,0:T(8,128)(2,1)} %get-tuple-element.79.ra_ref, bf16[1024,128]{1,0:T(8,128)(2,1)} %get-tuple-element.78.rb_ref, ...), custom_call_target="tpu_custom_call" | custom-call | flops 60000002048 | bytes 50000000 | tf_op jit(solution)/shard_map/query_part/pallas_call | solution.py:128
  372.5 1.8 slice_bitcast_fusion
  374.3 2.3 slice_bitcast_fusion.5
  376.5 1.3 copy.115
  377.8 2.5 copy.97
  380.3 2.7 reshape.53
  383.0 1.9 copy.98
  384.9 1.8 reshape.54
  386.8 4.8 pad_maximum_fusion.1
  391.6 6.0 %copy.114 = bf16[64,128,192]{1,2,0:T(8,128)(2,1)} copy(bf16[64,128,192]{2,1,0:T(8,128)(2,1)} %pad_maximum_fusion.1) | data formatting | bytes 6291456
  397.5 2.8 copy.96
  400.3 2.1 reshape.52
  403.0 1.3 reduce
  404.5 0.7 reduce_sum.8
  405.1 19.7 %weight_part.4 = (f32[512,128,128]{2,1,0:T(8,128)}, f32[512,128,128]{2,1,0:T(8,128)}, f32[64,512]{1,0:T(8,128)}) custom-call(bf16[16,2,1024,256]{3,2,1,0:T(8,128)(2,1)} %all-gather.8.cloned.1.call-done.refs_0_, bf16[512,1024]{1,0:T(8,128)(2,1)} %bitcast.50, bf16[128,512,128]{2,1,0:T(8,128)(2,1)} %get-tuple-element.82.wk_ref.refs_2_, ...), custom_call_target="tpu_custom_call" | custom-call | flops 8800000000 | bytes 40000000 | tf_op jit(solution)/shard_map/weight_part/pallas_call | solution.py:194
  424.9 19.9 %weight_part.5 = (f32[512,128,128]{2,1,0:T(8,128)}, f32[512,128,128]{2,1,0:T(8,128)}, f32[64,512]{1,0:T(8,128)}) custom-call(bf16[16,2,1024,256]{3,2,1,0:T(8,128)(2,1)} %all-gather.10.cloned.1.call-done.refs_0_, bf16[512,1024]{1,0:T(8,128)(2,1)} %bitcast.51, ...), custom_call_target="tpu_custom_call", output_to_operand_aliasing={{0}: (4, {}), {1}: (5, {})} | custom-call | flops 8800000000 | bytes 40000000 | tf_op jit(solution)/shard_map/weight_part/pallas_call | solution.py:194
  444.8 19.8 %weight_part.6 = (f32[512,128,128]{2,1,0:T(8,128)}, f32[512,128,128]{2,1,0:T(8,128)}, f32[64,512]{1,0:T(8,128)}) custom-call(bf16[16,2,1024,256]{3,2,1,0:T(8,128)(2,1)} %all-gather.12.cloned.1.call-done.refs_0_, bf16[512,1024]{1,0:T(8,128)(2,1)} %bitcast.52, ...), custom_call_target="tpu_custom_call", output_to_operand_aliasing={{0}: (4, {}), {1}: (5, {})} | custom-call | flops 8800000000 | bytes 40000000 | tf_op jit(solution)/shard_map/weight_part/pallas_call | solution.py:194
  464.6 19.8 %weight_part.7 = (f32[512,128,128]{2,1,0:T(8,128)}, f32[512,128,128]{2,1,0:T(8,128)}, f32[64,512]{1,0:T(8,128)}) custom-call(bf16[16,2,1024,256]{3,2,1,0:T(8,128)(2,1)} %all-gather.14.cloned.1.call-done.refs_0_, bf16[512,1024]{1,0:T(8,128)(2,1)} %bitcast.53, ...), custom_call_target="tpu_custom_call", output_to_operand_aliasing={{0}: (4, {}), {1}: (5, {})} | custom-call | flops 8800000000 | bytes 40000000 | tf_op jit(solution)/shard_map/weight_part/pallas_call | solution.py:194
  484.5 1.6 add_convert_fusion
  (44 shorter events, 1.5 us)
Async XLA Ops:
  7.2 1.6 slice-start
  11.6 4.2 copy-start.2
  11.6 6.3 %slice-start.1 = ((bf16[64,128,192]{1,2,0:T(8,128)(2,1)}), bf16[64,128,64]{1,2,0:T(8,128)(2,1)S(1)}, s32[]{:S(2)}) async-start(bf16[64,128,192]{1,2,0:T(8,128)(2,1)} %param.6), calls=%async_computation.11 | async-start | bytes 2097152 | tf_op jit(solution)/shard_map/slice | solution.py:224
  26.0 3.0 copy-start
  26.0 8.4 %copy-start.9 = (bf16[64,512]{1,0:T(8,128)(2,1)S(1)}, bf16[64,512]{1,0:T(8,128)(2,1)}, u32[]{:S(2)}) copy-start(bf16[64,512]{1,0:T(8,128)(2,1)} %param.7) | copy-start | bytes 196612
  26.0 8.4 %copy-start.10 = (bf16[64,64]{1,0:T(8,128)(2,1)S(1)}, bf16[64,64]{1,0:T(8,128)(2,1)}, u32[]{:S(2)}) copy-start(bf16[64,64]{1,0:T(8,128)(2,1)} %param.8) | copy-start | bytes 24580
  29.0 51.5 %all-to-all-start = ((bf16[16,1,64,640]{3,2,1,0:T(8,128)(2,1)}), bf16[16,1,64,640]{3,2,1,0:T(8,128)(2,1)}, u32[]{:S(2)}, u32[]{:S(2)}) async-start(bf16[16,1,64,640]{3,2,1,0:T(8,128)(2,1)} %get-tuple-element.74), calls=%async_computation | async-start | bytes 2621440 | tf_op jit(solution)/shard_map/all_to_all | solution.py:236
  34.3 42.0 %all-gather.6.cloned.1.call-start = ((), (), s32[]{:S(2)}) async-start(), calls=%async_computation.5 | async-start | bytes 1392640 | tf_op jit(solution)/shard_map/all_gather | solution.py:225
  35.1 370.0 %all-gather.8.cloned.1.call-start = ((), (), s32[]{:S(2)}) async-start(), calls=%async_computation.6 | async-start | bytes 17825792 | tf_op jit(solution)/shard_map/all_gather | solution.py:241
  88.6 336.3 %all-gather.10.cloned.1.call-start = ((), (), s32[]{:S(2)}) async-start(), calls=%async_computation.7 | async-start | bytes 17825792 | tf_op jit(solution)/shard_map/all_gather | solution.py:241
  127.0 317.8 %all-gather.12.cloned.1.call-start = ((), (), s32[]{:S(2)}) async-start(), calls=%async_computation.8 | async-start | bytes 17825792 | tf_op jit(solution)/shard_map/all_gather | solution.py:241
  161.9 302.7 %all-gather.14.cloned.1.call-start = ((), (), s32[]{:S(2)}) async-start(), calls=%async_computation.9 | async-start | bytes 17825792 | tf_op jit(solution)/shard_map/all_gather | solution.py:241
  197.8 8.2 %copy-start.3 = (f32[1,1024,128]{2,1,0:T(8,128)S(1)}, f32[1,1024,128]{2,1,0:T(8,128)}, u32[]{:S(2)}) copy-start(f32[1,1024,128]{2,1,0:T(8,128)} %get-tuple-element.44) | copy-start | bytes 1572868
  197.8 8.2 %copy-start.4 = (f32[1,1024,128]{2,1,0:T(8,128)S(1)}, f32[1,1024,128]{2,1,0:T(8,128)}, u32[]{:S(2)}) copy-start(f32[1,1024,128]{2,1,0:T(8,128)} %get-tuple-element.45) | copy-start | bytes 1572868
  197.8 8.2 %copy-start.5 = (f32[1,1024,128]{2,1,0:T(8,128)S(1)}, f32[1,1024,128]{2,1,0:T(8,128)}, u32[]{:S(2)}) copy-start(f32[1,1024,128]{2,1,0:T(8,128)} %get-tuple-element.46) | copy-start | bytes 1572868
  208.4 194.0 %all-to-all-start.4 = ((f32[16,1,4096]{2,1,0:T(1,128)}), f32[16,1,4096]{2,1,0:T(1,128)S(1)}, u32[]{:S(2)}, u32[]{:S(2)}) async-start(f32[16,1,4096]{2,1,0:T(1,128)} %reshape.56), calls=%async_computation.4 | async-start | bytes 524288 | tf_op jit(solution)/shard_map/all_to_all | solution.py:245
  372.5 4.1 copy-start.1
  464.6 19.9 %copy-start.6 = (f32[64,512]{1,0:T(8,128)S(1)}, f32[64,512]{1,0:T(8,128)}, u32[]{:S(2)}) copy-start(f32[64,512]{1,0:T(8,128)} %get-tuple-element.31) | copy-start | bytes 393220
  464.6 19.9 %copy-start.7 = (f32[64,512]{1,0:T(8,128)S(1)}, f32[64,512]{1,0:T(8,128)}, u32[]{:S(2)}) copy-start(f32[64,512]{1,0:T(8,128)} %get-tuple-element.35) | copy-start | bytes 393220
  464.6 19.9 %copy-start.8 = (f32[64,512]{1,0:T(8,128)S(1)}, f32[64,512]{1,0:T(8,128)}, u32[]{:S(2)}) copy-start(f32[64,512]{1,0:T(8,128)} %get-tuple-element.39) | copy-start | bytes 393220
Sparse Core Ops, SparseCore 0:
  37.4 29.5 all-gather.5
  88.7 113.9 all-gather.7
  204.9 77.9 all-gather.9
  285.0 76.2 all-gather.11
  363.4 76.0 all-gather.13

commit v2 on v0

v2 whole, which is shorter than its diff:
```python
import functools
import math
import jax
import jax.numpy as jnp
from jax import lax
from jax.experimental import pallas as pl
from jax.experimental.pallas import tpu as pltpu
from jax.sharding import PartitionSpec as P

N_DEV = 16
TOK = 64
SEQ = 1024
PAIRS = 64
OWN = 4
Q_BLK = 256
LOG2E = 1.4426950408889634
F32 = jnp.float32
BF16 = jnp.bfloat16
MESH = pl.DeviceIdType.MESH
CORE, AX, AY, AZ = 1, 2, 4, 8
ORDERS = ((AX, AY, AZ), (AY, AZ, AX), (AZ, AX, AY))
ROWS = ((0, 336), (336, 336), (672, 352))
CHIPS = (0, 2, 4, 6, 8, 10, 12, 14)


def dot(a, b):
    return lax.dot_general(a, b, (((1,), (0,)), ((), ())), preferred_element_type=F32)


def dot_t(a, b):
    return lax.dot_general(a, b, (((1,), (1,)), ((), ())), preferred_element_type=F32)


def flip(me, mask):
    out = me
    for bit in (1, 2, 4, 8):
        if mask & bit:
            out = out + bit - 2 * bit * ((me // bit) % 2)
    return out


def pack_kernel(q_ref, do_ref, pay_ref, qn_ref, qr_ref, ds_ref):
    step = pl.program_id(0)

    @pl.when(step == 0)
    def _():
        def token(t, carry):
            rows = pl.ds(pl.multiple_of(t * 128, 128), 128)
            qt = q_ref[t].astype(F32)
            qn_ref[rows, :] = qt[0:128, :].T
            qr_ref[rows, 0:64] = qt[128:192, :].T
            ds_ref[rows, :] = do_ref[t].astype(F32)
            return carry
        lax.fori_loop(0, TOK, token, 0, unroll=4)

    for p in range(8):
        head = (step * 8 + p) * 2
        rope = []
        for a in range(2):
            rows = pl.ds(head + a, TOK, stride=128)
            pay_ref[p, :, a * 128:(a + 1) * 128] = qn_ref[rows, :].astype(BF16)
            pay_ref[p, :, 256 + a * 128:384 + a * 128] = ds_ref[rows, :].astype(BF16)
            rope.append(qr_ref[rows, :][:, 0:64])
        pay_ref[p, :, 512:640] = jnp.concatenate(rope, axis=-1).astype(BF16)


def pack(q_t, d_out):
    return pl.pallas_call(
        pack_kernel,
        grid=(8,),
        in_specs=[
            pl.BlockSpec((TOK, 192, 128), lambda s: (0, 0, 0)),
            pl.BlockSpec((TOK, 128, 128), lambda s: (0, 0, 0)),
        ],
        out_specs=pl.BlockSpec((8, TOK, 640), lambda s: (s, 0, 0)),
        out_shape=jax.ShapeDtypeStruct((PAIRS, TOK, 640), BF16),
        scratch_shapes=[pltpu.VMEM((TOK * 128, 128), F32)] * 3,
        cost_estimate=pl.CostEstimate(flops=8_000_000_000, bytes_accessed=11_000_000, transcendentals=0),
        name="pack",
    )(q_t, d_out)


def head_pair(scale, pp, x, c, ropes, wk, wv, out, dr_ref, kx_ref, v_ref, q_ref, p_ref, ds_ref):
    n_blk = SEQ // Q_BLK
    scale2 = scale * LOG2E
    k_all = dot(c, wk).astype(BF16)
    v_ref[...] = dot(c, wv).astype(BF16)
    lane = lax.broadcasted_iota(jnp.int32, (Q_BLK, 128), 1)
    key = lax.broadcasted_iota(jnp.int32, (Q_BLK, Q_BLK), 0)
    qry = lax.broadcasted_iota(jnp.int32, (Q_BLK, Q_BLK), 1)
    for a in range(2):
        cols = slice(a * 128, (a + 1) * 128)
        kx_ref[...] = jnp.concatenate([k_all[:, cols], ropes[a]], axis=-1)
        q_ref[...] = jnp.concatenate([x[:, cols], x[:, 512:640]], axis=-1)
        do = x[:, 256 + a * 128:384 + a * 128]
        for i in range(n_blk):
            top = (i + 1) * Q_BLK
            rows = slice(i * Q_BLK, top)
            s = dot_t(kx_ref[:top, :], q_ref[rows, :]) * scale2
            diag = jnp.where(key <= qry, s[i * Q_BLK:, :], -1e30)
            s = diag if i == 0 else jnp.concatenate([s[:i * Q_BLK, :], diag], axis=0)
            e = jnp.exp2(s - jnp.max(s, axis=0, keepdims=True))
            p = e / jnp.sum(e, axis=0, keepdims=True)
            dp = dot_t(v_ref[:top, cols], do[rows, :])
            delta = jnp.sum(p * dp, axis=0, keepdims=True)
            p_ref[:top, rows] = p.astype(BF16)
            ds_ref[:top, rows] = (p * (dp - delta) * scale).astype(BF16)
        for j in range(n_blk):
            rows = slice(j * Q_BLK, (j + 1) * Q_BLK)
            out[1, rows, cols] = dot(p_ref[rows, j * Q_BLK:], do[j * Q_BLK:, :]).astype(BF16)
            dk = dot(ds_ref[rows, j * Q_BLK:], q_ref[j * Q_BLK:, :])
            out[0, rows, cols] = dk[:, :128].astype(BF16)
            keep = lane < 64 if a == 0 else lane >= 64
            dr_ref[rows, :] = dr_ref[rows, :] + jnp.where(keep, dk[:, 128:], 0.0)


def query_pair(scale, me, x, c, ropes, wk, wv):
    scale2 = scale * LOG2E
    k_all = dot(c, wk).astype(BF16)
    v_all = dot(c, wv).astype(BF16)
    key = lax.broadcasted_iota(jnp.int32, (TOK, SEQ), 1)
    qry = lax.broadcasted_iota(jnp.int32, (TOK, SEQ), 0) + me * TOK
    outs, grads = [], []
    for a in range(2):
        cols = slice(a * 128, (a + 1) * 128)
        kx = jnp.concatenate([k_all[:, cols], ropes[a]], axis=-1)
        q = jnp.concatenate([x[:, cols], x[:, 512:640]], axis=-1)
        do = x[:, 256 + a * 128:384 + a * 128]
        s = jnp.where(key <= qry, dot_t(q, kx) * scale2, -1e30)
        e = jnp.exp2(s - jnp.max(s, axis=1, keepdims=True))
        p = e / jnp.sum(e, axis=1, keepdims=True)
        v = v_all[:, cols]
        outs.append(dot(p.astype(BF16), v))
        dp = dot_t(do, v)
        ds = (p * (dp - jnp.sum(p * dp, axis=1, keepdims=True)) * scale).astype(BF16)
        grads.append(dot(ds, kx))
    return outs, grads


def mega_kernel(scale, pay, cr, wk, wv,
                dkv, wt_out, o_out, dq_out, dr_out, c_out,
                xbuf, cbuf, rb, wnat, wt, stage, kx, vs, qs, ps, dss, dr_acc, dr_land, xq, osc, dqn, dqr,
                c_send, c_recv, c_sib, x_send, x_recv, ici_send, ici_recv, sib_send, sib_recv,
                dr_send, dr_recv, load_sem, wsem, xq_sem, wt_sem, st_sem):
    me = lax.axis_index("cp")
    core = me % 2
    chip = me // 2
    sib = flip(me, CORE)
    bar = pltpu.get_barrier_semaphore()
    for m in range(1, N_DEV):
        pl.semaphore_signal(bar, inc=1, device_id=(flip(me, m),), device_id_type=MESH)
    pl.semaphore_wait(bar, N_DEV - 1)

    def remote(src, dst, ssem, rsem, to):
        return pltpu.make_async_remote_copy(src_ref=src, dst_ref=dst, send_sem=ssem, recv_sem=rsem,
                                            device_id=(to,), device_id_type=MESH)

    for m in CHIPS[1:]:
        remote(cr, cbuf.at[chip, core], c_send, c_recv, flip(me, m)).start()
    own_c = pltpu.make_async_copy(cr, cbuf.at[chip, core], load_sem.at[0])
    own_c.start()
    own_w = []
    for i, w in enumerate((wk, wv)):
        cp = pltpu.make_async_copy(w.at[:, pl.ds(pl.multiple_of(me * 8, 8), 8), :], wnat.at[0, i], wsem.at[0, i])
        cp.start()
        own_w.append(cp)
    for pp in range(OWN):
        for m in range(1, N_DEV):
            to = flip(me, m)
            remote(pay.at[OWN * to + pp], xbuf.at[pp, me], x_send, x_recv.at[pp], to).start()
    own_x = pltpu.make_async_copy(pay.at[pl.ds(OWN * me, OWN)], xbuf.at[:, me], load_sem.at[1])
    own_x.start()

    dr_acc[...] = jnp.zeros_like(dr_acc)
    for cp in own_w:
        cp.wait()
    for i in range(2):
        wt[0, i] = jnp.transpose(wnat[0, i], (1, 0, 2))
    own_c.wait()
    arrived = cbuf.at[pl.ds(0, 7), 0]
    pltpu.make_async_copy(arrived, arrived, c_recv).wait()
    fwd = remote(cbuf.at[:, core], cbuf.at[:, core], c_send, c_sib, sib)
    fwd.start()
    fwd.wait_recv()

    def latent():
        return cbuf[...].reshape(SEQ, 640)

    rope_a = latent()[:, 512:640].astype(F32)
    rb[...] = pltpu.roll(rope_a, 64, axis=1).astype(BF16)

    def operands():
        cc = latent()
        return cc[:, :512], (cc[:, 512:640], rb[...])

    own_x.wait()

    def block(mask, p, k):
        return dkv.at[OWN * flip(me, mask) + p, :, pl.ds(ROWS[k][0], ROWS[k][1]), :]

    def to_sibling(mask, p, k):
        b = block(mask, p, k)
        remote(b, b, sib_send, sib_recv, sib).start()

    def known(k, s):
        masks = [0]
        for d in ORDERS[k][:s]:
            masks = masks + [m + d for m in masks]
        return masks

    def gather_stage(p, s):
        for k in range(3):
            if s > 0:
                d = ORDERS[k][s - 1]
                for m in known(k, s - 1):
                    b = block(m + d, p, k)
                    pltpu.make_async_copy(b, b, ici_recv.at[p, k, (m + d) // 2]).wait()
            if s < 3:
                d = ORDERS[k][s]
                for m in known(k, s):
                    b = block(m, p, k)
                    remote(b, b, ici_send, ici_recv.at[p, k, (m + d) // 2], flip(me, d)).start()
        for k in range(3):
            fresh = [0] if s == 0 else [m + ORDERS[k][s - 1] for m in known(k, s - 1)]
            for m in fresh:
                to_sibling(m, p, k)

    def head_step(pp, carry):
        got = xbuf.at[pp, pl.ds(0, N_DEV - 1)]
        pltpu.make_async_copy(got, got, x_recv.at[pp]).wait()
        x = xbuf[pp].reshape(SEQ, 640)
        c, ropes = operands()
        wkp = jnp.concatenate([wt[0, 0, 2 * pp], wt[0, 0, 2 * pp + 1]], axis=-1)
        wvp = jnp.concatenate([wt[0, 1, 2 * pp], wt[0, 1, 2 * pp + 1]], axis=-1)
        head_pair(scale, pp, x, c, ropes, wkp, wvp, stage, dr_acc, kx, vs, qs, ps, dss)
        cp = pltpu.make_async_copy(stage, dkv.at[OWN * me + pp], st_sem)
        cp.start()
        cp.wait()
        for p in range(OWN):
            @pl.when(pp == p)
            def _():
                gather_stage(p, 0)
        return carry

    lax.fori_loop(0, OWN, head_step, 0)

    for m in range(1, N_DEV):
        to = flip(me, m)
        remote(dr_acc.at[pl.ds(pl.multiple_of(to * TOK, TOK), TOK), :], dr_land.at[me], dr_send, dr_recv, to).start()
    own_dr = pltpu.make_async_copy(dr_acc.at[pl.ds(pl.multiple_of(me * TOK, TOK), TOK), :], dr_out, load_sem.at[2])
    own_dr.start()

    def fetch(g, slot):
        cps = [pltpu.make_async_copy(w.at[:, pl.ds(pl.multiple_of(g * 8, 8), 8), :], wnat.at[slot, i], wsem.at[slot, i])
               for i, w in enumerate((wk, wv))]
        cps.append(pltpu.make_async_copy(pay.at[pl.ds(g * 4, 4)], xq.at[slot], xq_sem.at[slot]))
        return cps

    def put_w(g, slot):
        return pltpu.make_async_copy(wt.at[slot], wt_out.at[:, pl.ds(pl.multiple_of(g * 8, 8), 8)], wt_sem.at[slot])

    for cp in fetch(0, 0):
        cp.start()

    plan = {0: ((0, 1),), 1: ((1, 1),), 2: ((2, 1),), 4: ((0, 2),), 6: ((3, 1),), 8: ((1, 2),), 10: ((2, 2),), 12: ((3, 2),)}

    def query_step(g, carry):
        slot = g % 2
        for cp in fetch(g, slot):
            cp.wait()

        @pl.when(g < 15)
        def _():
            for cp in fetch(g + 1, 1 - slot):
                cp.start()

        @pl.when(g >= 2)
        def _():
            put_w(g - 2, slot).wait()

        for i in range(2):
            wt[slot, i] = jnp.transpose(wnat[slot, i], (1, 0, 2))
        put_w(g, slot).start()

        def pair_step(j, carry):
            x = xq[slot, j]
            c, ropes = operands()
            wkp = jnp.concatenate([wt[slot, 0, 2 * j], wt[slot, 0, 2 * j + 1]], axis=-1)
            wvp = jnp.concatenate([wt[slot, 1, 2 * j], wt[slot, 1, 2 * j + 1]], axis=-1)
            outs, grads = query_pair(scale, me, x, c, ropes, wkp, wvp)
            for a in range(2):
                osc[pl.ds(2 * j + a, TOK, stride=8), :] = outs[a]
                rows = pl.ds(g * 8 + 2 * j + a, TOK, stride=128)
                dqn[rows, :] = grads[a][:, :128]
                rope = grads[a][:, 128:]
                dqr[rows, :] = rope if a == 0 else pltpu.roll(rope, 64, axis=1)
            return carry

        lax.fori_loop(0, 4, pair_step, 0)
        o_out[:, pl.ds(pl.multiple_of(g * 8, 8), 8), :] = osc[...].reshape(TOK, 8, 128).astype(BF16)
        for when, events in plan.items():
            @pl.when(g == when)
            def _():
                for p, s in events:
                    gather_stage(p, s)
        return carry

    lax.fori_loop(0, 16, query_step, 0)

    def dq_token(t, carry):
        rows = pl.ds(pl.multiple_of(t * 128, 128), 128)
        dq_out[t, 0:128, :] = dqn[rows, :].T.astype(BF16)
        dq_out[t, 128:192, :] = dqr[rows, :].T[0:64, :].astype(BF16)
        return carry

    lax.fori_loop(0, TOK, dq_token, 0)
    c_out[...] = latent()[:, :512]
    for p in range(OWN):
        gather_stage(p, 3)

    own_dr.wait()
    got = dr_land.at[pl.ds(0, N_DEV - 1)]
    pltpu.make_async_copy(got, got, dr_recv).wait()
    total = dr_out[...]
    for m in range(1, N_DEV):
        total = total + dr_land[flip(me, m)]
    dr_out[...] = total

    put_w(14, 0).wait()
    put_w(15, 1).wait()
    pltpu.make_async_copy(got, got, dr_send).wait()
    got = xbuf.at[:, pl.ds(0, N_DEV - 1)]
    pltpu.make_async_copy(got, got, x_send).wait()
    arrived = cbuf.at[pl.ds(0, 7), 0]
    pltpu.make_async_copy(arrived, arrived, c_send).wait()
    arrived = cbuf.at[:, 0]
    pltpu.make_async_copy(arrived, arrived, c_send).wait()
    sent = dkv.at[pl.ds(0, 7 * OWN)]
    pltpu.make_async_copy(sent, sent, ici_send).wait()
    sent = dkv.at[pl.ds(0, 8 * OWN)]
    pltpu.make_async_copy(sent, sent, sib_send).wait()
    pltpu.make_async_copy(sent, sent, sib_recv).wait()


def mega(scale, pay, cr, wk, wv):
    any_spec = pl.BlockSpec(memory_space=pl.ANY)
    vmem = pl.BlockSpec(memory_space=pltpu.VMEM)
    dma = pltpu.SemaphoreType.DMA
    return pl.pallas_call(
        functools.partial(mega_kernel, scale),
        in_specs=[any_spec] * 4,
        out_specs=[any_spec, any_spec, vmem, vmem, vmem, vmem],
        out_shape=[
            jax.ShapeDtypeStruct((PAIRS, 2, SEQ, 256), BF16),
            jax.ShapeDtypeStruct((2, 128, 512, 128), BF16),
            jax.ShapeDtypeStruct((TOK, 128, 128), BF16),
            jax.ShapeDtypeStruct((TOK, 192, 128), BF16),
            jax.ShapeDtypeStruct((TOK, 128), F32),
            jax.ShapeDtypeStruct((SEQ, 512), BF16),
        ],
        scratch_shapes=[
            pltpu.VMEM((OWN, N_DEV, TOK, 640), BF16),
            pltpu.VMEM((8, 2, TOK, 640), BF16),
            pltpu.VMEM((SEQ, 128), BF16),
            pltpu.VMEM((2, 2, 512, 8, 128), BF16),
            pltpu.VMEM((2, 2, 8, 512, 128), BF16),
            pltpu.VMEM((2, SEQ, 256), BF16),
            pltpu.VMEM((SEQ, 256), BF16), pltpu.VMEM((SEQ, 256), BF16), pltpu.VMEM((SEQ, 256), BF16),
            pltpu.VMEM((SEQ, SEQ), BF16), pltpu.VMEM((SEQ, SEQ), BF16),
            pltpu.VMEM((SEQ, 128), F32),
            pltpu.VMEM((N_DEV, TOK, 128), F32),
            pltpu.VMEM((2, 4, TOK, 640), BF16),
            pltpu.VMEM((TOK * 8, 128), F32),
            pltpu.VMEM((TOK * 128, 128), F32), pltpu.VMEM((TOK * 128, 128), F32),
            dma, dma, dma, dma, dma((OWN,)), dma, dma((OWN, 3, 8)), dma, dma,
            dma, dma, dma((3,)), dma((2, 2)), dma((2,)), dma((2,)), dma,
        ],
        compiler_params=pltpu.CompilerParams(collective_id=0, has_side_effects=True, vmem_limit_bytes=60 * 1024 * 1024),
        cost_estimate=pl.CostEstimate(flops=100_000_000_000, bytes_accessed=200_000_000, transcendentals=0),
        name="mega",
    )(pay, cr, wk, wv)


def weight_kernel(dkv_ref, ct_ref, wt_ref, dwk_ref, dwv_ref, dc_ref):
    me = lax.axis_index("cp")
    n_pair = dkv_ref.shape[0]
    own = pl.ds(pl.multiple_of(me * TOK, TOK), TOK)
    dc = jnp.zeros(dc_ref.shape, F32)
    for which, out_ref in enumerate((dwk_ref, dwv_ref)):
        flat = out_ref.reshape(512 * 8, 128)
        for p in range(n_pair):
            g = dkv_ref[p, which]
            for m in range(2):
                res = dot(ct_ref[m * 256:(m + 1) * 256, :], g)
                for a in range(2):
                    flat[pl.ds(m * 2048 + 2 * p + a, 256, stride=8), :] = res[:, a * 128:(a + 1) * 128]
            mine = dkv_ref[p, which, own, :]
            dc += dot_t(mine, jnp.concatenate([wt_ref[which, 2 * p], wt_ref[which, 2 * p + 1]], axis=-1))

    @pl.when(pl.program_id(0) == 0)
    def _():
        dc_ref[...] = dc

    @pl.when(pl.program_id(0) > 0)
    def _():
        dc_ref[...] += dc


def weight_part(dkv, ct, wt):
    out_block = pl.BlockSpec((512, 8, 128), lambda g: (0, g, 0))
    return pl.pallas_call(
        weight_kernel,
        grid=(PAIRS // 4,),
        in_specs=[
            pl.BlockSpec((4, 2, SEQ, 256), lambda g: (g, 0, 0, 0)),
            pl.BlockSpec((512, SEQ), lambda g: (0, 0)),
            pl.BlockSpec((2, 8, 512, 128), lambda g: (0, g, 0, 0)),
        ],
        out_specs=[out_block, out_block, pl.BlockSpec((TOK, 512), lambda g: (0, 0))],
        out_shape=[
            jax.ShapeDtypeStruct((512, 128, 128), F32),
            jax.ShapeDtypeStruct((512, 128, 128), F32),
            jax.ShapeDtypeStruct((TOK, 512), F32),
        ],
        cost_estimate=pl.CostEstimate(flops=36_000_000_000, bytes_accessed=170_000_000, transcendentals=0),
        name="weight_part",
    )(dkv, ct, wt)


def solution(mesh):
    seq_spec = P("cp")

    def local_step(queries, latent, key_rope, w_uk, w_uv, d_out):
        scale = 1.0 / math.sqrt(queries.shape[-1])
        pay = pack(queries.transpose(0, 2, 1), d_out)
        cr = jnp.concatenate([latent, key_rope, jnp.zeros_like(key_rope)], axis=-1)
        dkv, wt, o, dq, dr, c_all = mega(scale, pay, cr, w_uk, w_uv)
        dwk, dwv, dc = weight_part(dkv, c_all.T, wt)
        d_key_rope = (dr[:, :64] + dr[:, 64:]).astype(BF16)
        return o, dq.transpose(0, 2, 1), dc.astype(BF16), d_key_rope, dwk, dwv

    return jax.shard_map(local_step, mesh=mesh,
                         in_specs=(seq_spec, seq_spec, seq_spec, P(), P(), seq_spec),
                         out_specs=(seq_spec, seq_spec, seq_spec, seq_spec, P(), P()),
                         check_vma=False)
```

time: 1720 us -> 395 us (0.23)
  waiting for transfers between devices: 1250 us -> 0 us
  Pallas kernels: 0 us -> 384 us
  matrix products: 255 us -> 0 us
  local copies, waits for them, and re-layouts: 148 us -> 5.33 us
  other arithmetic: 23.6 us -> 4.72 us
    reduce_scatter x3 -> x0, waiting for transfers between devices: 600 us -> none  [the longest x1 331 us: local_step(): d_k_nope = lax.psum_scatter(dk_part, 'cp', scatter_dimension=0, tiled=True)]
    psum x1 -> x0, waiting for transfers between devices: 508 us -> none  [local_step(): lax.psum(jnp.einsum('tl,thd->lhd', latent, d_k_nope, preferred_element_ty...]
    pallas_call x0 -> x3, Pallas kernels: none -> 384 us  [the longest x1 300 us: mega(): pl.pallas_call(functools.partial(mega_kernel, scale), in_specs=[any_spec]...]
    dot_general x15 -> x0, matrix products: 255 us -> none  [the longest x1 29.4 us: local_step(): jnp.einsum('qhd,khd->hqk', d_out, v_all, preferred_element_type=jnp.float32)]
    all_gather x2 -> x0, waiting for transfers between devices: 142 us -> none  [the longest x1 83.7 us: gather_all(): k_all = lax.all_gather(k_nope, 'cp', tiled=True)]
    unnamed x25 -> x6, local copies, waits for them, and re-layouts: 134 us -> 2.99 us
  transfers between devices with their start and end apart: 6 -> 0, of which waited for: 5 -> 0; matrix products, arithmetic and copies ran while one was open for 22% -> 0% of each run, Pallas kernels for 0% -> 0%
where the time goes in v2:
time: 395 us
  Pallas kernels  384 us (97%)
  local copies, waits for them, and re-layouts  5.33 us (1%)
  other arithmetic  4.72 us (1%)
    pallas_call x1, Pallas kernels, mega(): pl.pallas_call(functools.partial(mega_kernel, scale), in_specs=[any_spec]...  300 us
    pallas_call x1, Pallas kernels, weight_part(): pl.pallas_call(weight_kernel, grid=(PAIRS // 4,), in_specs=[pl.BlockSpec(...  69.5 us
    pallas_call x1, Pallas kernels, pack(): pl.pallas_call(pack_kernel, grid=(8,), in_specs=[pl.BlockSpec((TOK, 192,...  15.2 us

profile of v2, /device:TPU:0, one launch (start us, length us, event | category | flops | bytes accessed | tf_op | source)
XLA Modules:
  0.0 395.0 jit_solution(1781987807027143031)
XLA Ops:
  0.6 0.1 pad.2.clone
  0.7 1.5 maximum_maximum_fusion.cr
  2.2 15.2 %pack.1.pay = bf16[64,64,640]{2,1,0:T(8,128)(2,1)} custom-call(bf16[64,192,128]{2,1,0:T(8,128)(2,1)} %bitcast.5, bf16[64,128,128]{2,1,0:T(8,128)(2,1)} %do_ref.1), custom_call_target="tpu_custom_call" | custom-call | flops 8000000000 | bytes 11000000 | tf_op jit(solution)/shard_map/pack/pallas_call | solution.py:68
  17.5 299.6 %mega.1 = (bf16[64,2,1024,256]{3,2,1,0:T(8,128)(2,1)}, bf16[2,128,512,128]{3,2,1,0:T(8,128)(2,1)}, bf16[64,128,128]{2,1,0:T(8,128)(2,1)}, bf16[64,192,128]{2,1,0...) custom-call(bf16[64,64,640]{2,1,0:T(8,128)(2,1)} %pack.1.pay, bf16[64,640]{1,0:T(8,128)(2,1)} %maximum_maximum_fusion.cr, ...), custom_call_target="tpu_custom_call" | custom-call | flops 99999997952 | bytes 200000000 | tf_op jit(solution)/shard_map/mega/pallas_call | solution.py:349
  317.0 1.5 add_convert_fusion
  318.6 2.3 copy.12
  320.8 0.0 copy-start.1
  320.8 69.5 %weight_part.1 = (f32[512,128,128]{2,1,0:T(8,128)}, f32[512,128,128]{2,1,0:T(8,128)}, f32[64,512]{1,0:T(8,128)}) custom-call(bf16[64,2,1024,256]{3,2,1,0:T(8,128)(2,1)} %get-tuple-element.17.dkv_ref, bf16[512,1024]{1,0:T(8,128)(2,1)} %bitcast.4, bf16[2,128,512,128]{3,2,1,0:T(8,128)(2,1)} %get-tuple-element.19.wt_ref), custom_call_target="tpu_custom_call" | custom-call | flops 35999997952 | bytes 170000000 | tf_op jit(solution)/shard_map/weight_part/pallas_call | solution.py:411
  390.4 0.0 copy-start
  390.4 1.7 convert_element_type.6
  392.1 0.0 copy-done.1
  392.1 1.3 copy.15
  393.4 0.0 copy-done
  393.4 1.7 copy.16
  (1 shorter events, 0.0 us)
Async XLA Ops:
  320.8 71.2 %copy-start.1 = (bf16[64,128,128]{2,1,0:T(8,128)(2,1)S(1)}, bf16[64,128,128]{2,1,0:T(8,128)(2,1)}, u32[]{:S(2)}) copy-start(bf16[64,128,128]{2,1,0:T(8,128)(2,1)} %get-tuple-element.30) | copy-start | bytes 6291460
  390.4 3.0 copy-start
